TPU v7x, 32 devices: a whole 2x2x4 slice. The times are simulated.
32 devices in a mesh: lat: 8 (over z, y), lon: 4 (over x, core).
Axes of the slice: x: 2, y: 2, z: 4, core: 2. Of those that a mesh axis runs over, the one named last changes fastest.
Arguments:
- grid_latent: bfloat16 [16384, 512], P(('lat', 'lon')), may hold values from -6 to 6
- grid_feat: bfloat16 [4, 65536], P(None, ('lat', 'lon')), may hold values from -6 to 6
- grid_sender: int32 [65536], P(('lat', 'lon')), may hold values from 0 to 511
- grid_owner: int32 [65536, 1], P(('lat', 'lon')), may hold values from 0 to 7; in each aligned block of 2048 rows (0 to 2047, 2048 to 4095, ...) at most 512 rows name the same one
- grid_node: int32 [65536], P(('lat', 'lon')), may hold values from 0 to 511
- mesh_latent: bfloat16 [4096, 512], P('lat', 'lon'), may hold values from -6 to 6
- mesh_edge: bfloat16 [32768, 512], P(('lat', 'lon')), may hold values from -6 to 6
- halo_send: int32 [64, 64], P('lat'), may hold values from 0 to 511
- mesh_sender: int32 [32768], P(('lat', 'lon')), may hold values from 0 to 1023
- mesh_receiver: int32 [32768], P(('lat', 'lon')), may hold values from 0 to 511
- enc_edge_in: bfloat16 [512, 512], P(None, 'lon'), may hold values from -0.25 to 0.25
- enc_feat_proj: bfloat16 [4, 512], replicated, may hold values from -3 to 3
- enc_edge_out: bfloat16 [512, 512], P(None, 'lon'), may hold values from -0.25 to 0.25
- enc_edge_bias: float32 [2, 512], replicated, may hold values from -1.5 to 1.5
- enc_edge_gain: float32 [512], replicated, may hold values from 0.25 to 1.75
- enc_node_in: bfloat16 [1024, 512], P(None, 'lon'), may hold values from -0.1875 to 0.1875
- enc_node_out: bfloat16 [512, 512], P('lon'), may hold values from -0.25 to 0.25
- enc_node_bias: float32 [2, 512], replicated, may hold values from -1.5 to 1.5
- enc_node_gain: float32 [512], replicated, may hold values from 0.25 to 1.75
- proc_edge_in: bfloat16 [1536, 512], P(None, 'lon'), may hold values from -0.15625 to 0.15625
- proc_edge_out: bfloat16 [512, 512], P(None, 'lon'), may hold values from -0.25 to 0.25
- proc_edge_bias: float32 [2, 512], replicated, may hold values from -1.5 to 1.5
- proc_edge_gain: float32 [512], replicated, may hold values from 0.25 to 1.75
- proc_node_in: bfloat16 [1024, 512], P(None, 'lon'), may hold values from -0.1875 to 0.1875
- proc_node_out: bfloat16 [512, 512], P('lon'), may hold values from -0.25 to 0.25
- proc_node_bias: float32 [2, 512], replicated, may hold values from -1.5 to 1.5
- proc_node_gain: float32 [512], replicated, may hold values from 0.25 to 1.75
Outputs:
- mesh_update: bfloat16 [4096, 512], P('lat', 'lon')
- edge_update: bfloat16 [32768, 512], P(('lat', 'lon'))
Inputs may be any that keep to these rules, and one draw needn't show every extreme that they name: `grid_sender`: a row among the 512 grid rows of the device that holds the edge. `grid_owner`: among the 2048 edges of one device, at most 512 name the same partition, a bound that some block reaches. `halo_send`: nodes of the listing partition.
All inputs are finite; a program needn't handle non-finite values.
Results may differ from a plain program's by a relative error of at most 0.017.
Values may be sent and summed in bfloat16 or wider, within the bound.
No kernel may reach another device: no remote copies, remote signals or barrier semaphores. Data moves between devices by JAX's collectives and lax.ppermute only.
A program may use at most 128 MiB of HBM per device.

v0:
```python
import jax
import jax.numpy as jnp
from jax import lax
from jax.sharding import PartitionSpec as P


def layer_norm(values, norm_gain, offsets):
    average = jnp.mean(values, axis=-1, keepdims=True)
    centred = values - average
    spread = jnp.mean(centred * centred, axis=-1, keepdims=True)
    return centred * lax.rsqrt(spread + 1e-05) * norm_gain + offsets


def encoder_edges(source_rows, feat_term, weight_in, weight_out):
    piece_in = lax.all_gather(weight_in, "lon", axis=1, tiled=True)
    piece_out = lax.all_gather(weight_out, "lon", axis=1, tiled=True)
    pre_act = jnp.dot(source_rows, piece_in, preferred_element_type=jnp.float32)
    pre_act = pre_act + feat_term
    hidden = jax.nn.silu(pre_act).astype(jnp.bfloat16)
    return lax.dot_general(
        hidden, piece_out, (((1,), (1,)), ((), ())), preferred_element_type=jnp.float32
    )


def node_network(base, aggregate, weight_in, weight_out, biases, norm_gain):
    inputs = jnp.concatenate([base, aggregate], 1)
    columns = weight_in.shape[1]
    hidden_bias = lax.dynamic_slice_in_dim(biases[0], lax.axis_index("lon") * columns, columns)
    hidden = jax.nn.silu(
        jnp.dot(inputs, weight_in, preferred_element_type=jnp.float32) + hidden_bias
    ).astype(jnp.bfloat16)
    raw_out = lax.psum(
        jnp.dot(hidden, weight_out, preferred_element_type=jnp.float32).astype(jnp.bfloat16), "lon"
    ).astype(jnp.float32)
    return (base.astype(jnp.float32) + layer_norm(raw_out, norm_gain, biases[1])).astype(
        jnp.bfloat16
    )


def local(
    grid_latent,
    grid_feat,
    grid_sender,
    grid_owner,
    grid_node,
    mesh_latent,
    mesh_edge,
    halo_send,
    mesh_sender,
    mesh_receiver,
    enc_edge_in,
    enc_feat_proj,
    enc_edge_out,
    enc_edge_bias,
    enc_edge_gain,
    enc_node_in,
    enc_node_out,
    enc_node_bias,
    enc_node_gain,
    proc_edge_in,
    proc_edge_out,
    proc_edge_bias,
    proc_edge_gain,
    proc_node_in,
    proc_node_out,
    proc_node_bias,
    proc_node_gain,
):
    lat_count = lax.axis_size("lat")
    lon_index = lax.axis_index("lon")
    feature_width = grid_latent.shape[1]
    quarter = mesh_latent.shape[1]
    mesh_rows = mesh_latent.shape[0]
    edge_count = grid_sender.shape[0]
    capacity = max(2, 2 * edge_count // lat_count)
    slot_total = lat_count * capacity
    owners = grid_owner[:, 0]
    owner_hits = (owners[:, None] == jnp.arange(lat_count, dtype=jnp.int32)[None, :]).astype(
        jnp.int32
    )
    slot_rank = jnp.sum((jnp.cumsum(owner_hits, axis=0) - owner_hits) * owner_hits, axis=1)
    slot_index = owners * capacity + slot_rank
    node_slots = (
        jnp.full((slot_total,), -1, jnp.int32)
        .at[slot_index]
        .set(grid_node)
        .reshape(lat_count, capacity)
    )
    row_buffer = (
        jnp.zeros((slot_total, feature_width), jnp.bfloat16)
        .at[slot_index]
        .set(grid_latent[grid_sender])
    )
    feat_buffer = (
        jnp.zeros((slot_total, grid_feat.shape[0]), jnp.bfloat16).at[slot_index].set(grid_feat.T)
    )
    got_rows, got_feats, node_ids = (
        lax.all_to_all(
            row_buffer.reshape(lat_count, capacity, feature_width),
            "lat",
            split_axis=0,
            concat_axis=0,
            tiled=True,
        ),
        lax.all_to_all(
            feat_buffer.reshape(lat_count, capacity, grid_feat.shape[0]),
            "lat",
            split_axis=0,
            concat_axis=0,
            tiled=True,
        ),
        lax.all_to_all(node_slots, "lat", split_axis=0, concat_axis=0, tiled=True),
    )
    got_rows = got_rows.reshape(slot_total, feature_width)
    got_feats = got_feats.reshape(slot_total, grid_feat.shape[0])
    feat_term = (
        jnp.dot(got_feats, enc_feat_proj, preferred_element_type=jnp.float32) + enc_edge_bias[0]
    )
    raw_out = encoder_edges(got_rows, feat_term, enc_edge_in, enc_edge_out)
    arrived = layer_norm(raw_out, enc_edge_gain, enc_edge_bias[1])
    node_ids = node_ids.reshape(slot_total)
    segment_ids = jnp.where(node_ids < 0, mesh_rows, node_ids).astype(jnp.int32)
    partial_sum = jax.ops.segment_sum(arrived, segment_ids, num_segments=mesh_rows + 1)[:mesh_rows]
    gathered = lax.psum(partial_sum.astype(jnp.bfloat16), "lon")
    mesh_full = lax.all_gather(mesh_latent, "lon", axis=1, tiled=True)
    mesh_mid = node_network(
        mesh_full, gathered, enc_node_in, enc_node_out, enc_node_bias, enc_node_gain
    )
    outgoing = mesh_mid[halo_send]
    received = lax.all_to_all(outgoing, "lat", split_axis=0, concat_axis=0, tiled=True)
    table = jnp.concatenate([mesh_mid, received.reshape(-1, feature_width)], 0)
    sender_rows = table[mesh_sender]
    receiver_rows = mesh_mid[mesh_receiver]
    piece_in = lax.all_gather(proc_edge_in, "lon", axis=1, tiled=True)
    piece_out = lax.all_gather(proc_edge_out, "lon", axis=1, tiled=True)
    pre_act = jnp.dot(mesh_edge, piece_in[:feature_width], preferred_element_type=jnp.float32)
    pre_act = pre_act + jnp.dot(
        sender_rows, piece_in[feature_width : 2 * feature_width], preferred_element_type=jnp.float32
    )
    pre_act = pre_act + jnp.dot(
        receiver_rows, piece_in[2 * feature_width :], preferred_element_type=jnp.float32
    )
    pre_act = pre_act + proc_edge_bias[0]
    hidden = jax.nn.silu(pre_act).astype(jnp.bfloat16)
    edge_raw = lax.dot_general(
        hidden, piece_out, (((1,), (1,)), ((), ())), preferred_element_type=jnp.float32
    )
    edge_update = (
        mesh_edge.astype(jnp.float32) + layer_norm(edge_raw, proc_edge_gain, proc_edge_bias[1])
    ).astype(jnp.bfloat16)
    edge_onehot = (
        jnp.arange(mesh_rows, dtype=jnp.int32)[:, None] == mesh_receiver[None, :]
    ).astype(jnp.bfloat16)
    incoming = lax.psum(
        jnp.dot(edge_onehot, edge_update, preferred_element_type=jnp.float32).astype(jnp.bfloat16),
        "lon",
    )
    mesh_new = node_network(
        mesh_mid, incoming, proc_node_in, proc_node_out, proc_node_bias, proc_node_gain
    )
    mesh_update = lax.dynamic_slice_in_dim(mesh_new, lon_index * quarter, quarter, 1)
    return (mesh_update, edge_update)


def solution(mesh):
    placed = (
        P(("lat", "lon"), None),
        P(None, ("lat", "lon")),
        P(("lat", "lon")),
        P(("lat", "lon"), None),
        P(("lat", "lon")),
        P("lat", "lon"),
        P(("lat", "lon"), None),
        P("lat", None),
        P(("lat", "lon")),
        P(("lat", "lon")),
        P(None, "lon"),
        P(),
        P(None, "lon"),
        P(),
        P(),
        P(None, "lon"),
        P("lon", None),
        P(),
        P(),
        P(None, "lon"),
        P(None, "lon"),
        P(),
        P(),
        P(None, "lon"),
        P("lon", None),
        P(),
        P(),
    )
    return jax.shard_map(
        local,
        mesh=mesh,
        in_specs=placed,
        out_specs=(P("lat", "lon"), P(("lat", "lon"), None)),
        check_vma=False,
    )
```

profile of v0, /device:TPU:0, one launch (start us, length us, event | category | flops | bytes accessed | tf_op | source)
XLA Modules:
  0.0 417.4 jit_solution(599329200880381121)
XLA Ops:
  12.2 8.8 %scatter_custom_fusion = s32[4096]{0:T(1024)} fusion(s32[2048]{0:T(1024)S(1)} %bitcast.71, s32[2048]{0:T(1024)} %param.31, s32[]{:T(128)} %constant.19.clone.1), kind=kCustom, calls=%fused_computation.87 | custom fusion | bytes 16896 | tf_op jit(solution)/shard_map/scatter | solution.py:86
  21.0 7.3 %all-to-all-start = ((s32[8,1,512]{2,1,0:T(1,128)}), s32[8,1,512]{2,1,0:T(1,128)S(1)}, u32[]{:S(2)}, u32[]{:S(2)}) async-start(s32[8,1,512]{2,1,0:T(1,128)} %bitcast.5), calls=%async_computation | async-start | bytes 32768 | tf_op jit(solution)/shard_map/all_to_all | solution.py:112
  29.0 21.3 %scatter_custom_fusion.1 = bf16[4096,512]{1,0:T(8,128)(2,1)} fusion(s32[2048]{0:T(1024)S(1)} %bitcast.72, bf16[512,512]{1,0:T(8,128)(2,1)S(1)} %copy-done, s32[2048]{0:T(1024)S(1)} %fusion.53, bf16[]{:T(256)} %constant.23.clone.1), kind=kCustom, calls=%fused_computation.11 | custom fusion | bytes 4194306 | tf_op jit(solution)/shard_map/scatter | solution.py:92
  50.3 6.1 %all-to-all-start.1 = ((bf16[8,512,512]{2,1,0:T(8,128)(2,1)}), bf16[8,512,512]{2,1,0:T(8,128)(2,1)}, u32[]{:S(2)}, u32[]{:S(2)}) async-start(bf16[8,512,512]{2,1,0:T(8,128)(2,1)} %bitcast.57), calls=%async_computation.1 | async-start | bytes 8388608 | tf_op jit(solution)/shard_map/all_to_all | solution.py:98
  56.8 6.1 %scatter_custom_fusion.2 = bf16[4096,4]{1,0:T(8,128)(2,1)S(1)} fusion(s32[2048]{0:T(1024)S(1)} %bitcast.73, bf16[2048,4]{1,0:T(8,128)(2,1)S(1)} %copy.41, bf16[]{:T(256)} %constant.23.clone.1), kind=kCustom, calls=%fused_computation.56 | custom fusion | bytes 32770 | tf_op jit(solution)/shard_map/scatter | solution.py:95
  63.9 7.2 %all_gather.16 = bf16[512,512]{1,0:T(8,128)(2,1)S(1)} all-gather(bf16[512,128]{1,0:T(8,128)(2,1)S(1)} %copy-done.8), channel_id=1, replica_groups=mesh['lat'=8,'lon'=4] {'lon'}, dimensions={1}, use_global_device_ids=true | all-gather | bytes 655360 | tf_op jit(solution)/shard_map/all_gather | solution.py:15
  71.1 7.3 %all_gather.17 = bf16[512,512]{1,0:T(8,128)(2,1)S(1)} all-gather(bf16[512,128]{1,0:T(8,128)(2,1)S(1)} %copy-done.9), channel_id=1, replica_groups=mesh['lat'=8,'lon'=4] {'lon'}, dimensions={1}, use_global_device_ids=true | all-gather | bytes 655360 | tf_op jit(solution)/shard_map/all_gather | solution.py:16
  78.4 70.7 %all-to-all-done.1 = bf16[8,512,512]{2,1,0:T(8,128)(2,1)} async-done(((bf16[8,512,512]{2,1,0:T(8,128)(2,1)}), bf16[8,512,512]{2,1,0:T(8,128)(2,1)}, u32[]{:S(2)}, u32[]{:S(2)}) %all-to-all-start.1) | async-done | bytes 4194336 | tf_op jit(solution)/shard_map/all_to_all | solution.py:98
  153.0 7.7 %fusion.76 = f32[4096,512]{1,0:T(8,128)} fusion(bf16[4096,512]{1,0:T(8,128)(2,1)} %bitcast.9, bf16[512,512]{1,0:T(8,128)(2,1)S(1)} %all_gather.16), kind=kOutput, calls=%fused_computation.114 | convolution fusion | flops 2147483648 | bytes 13107200 | tf_op jit(solution)/shard_map/dot_general | solution.py:17
  160.8 8.9 %fusion.72 = (f32[4096]{0:T(1024)S(1)}, f32[4096,512]{0,1:T(8,128)}) fusion(bf16[512,512]{1,0:T(8,128)(2,1)S(1)} %all_gather.17, f32[4096,512]{1,0:T(8,128)} %fusion.76, bf16[4096,4]{0,1:T(4,128)(2,1)S(1)} %bitcast.64, bf16[4,512]{1,0:T(4,128)(2,1)S(1)} %copy-done.27, f32[512]{0:T(512)S(1)} %bitcast.74), kind=kOutput, calls=%fused_computation.112 | convolution fusion | flops 2181033984 | bytes 17356800 | tf_op jit(solution)/shard_map/dot_general | solution.py:20
  169.7 4.5 %multiply_reduce_fusion = f32[4096]{0:T(1024)S(1)} fusion(f32[4096,512]{0,1:T(8,128)} %get-tuple-element.21, f32[4096]{0:T(1024)S(1)} %broadcast_multiply_fusion), kind=kLoop, calls=%fused_computation.9 | loop fusion | flops 6287360 | bytes 8421376 | tf_op jit(solution)/shard_map/reduce_sum | solution.py:10
  175.5 5.1 %multiply_add_fusion = f32[4096,512]{0,1:T(8,128)} fusion(f32[4096,512]{0,1:T(8,128)S(1)} %copy-done.2, f32[512]{0:T(512)S(1)} %bitcast.70, f32[512]{0:T(512)S(1)} %copy-done.21, f32[4096]{0:T(1024)S(1)} %add_rsqrt_fusion, f32[4096]{0:T(1024)S(1)} %broadcast_multiply_fusion), kind=kLoop, calls=%fused_computation.8 | loop fusion | flops 8388608 | bytes 16814080 | tf_op jit(solution)/shard_map/add | solution.py:11
  180.6 9.0 %copy.43 = f32[4096,512]{1,0:T(8,128)} copy(f32[4096,512]{0,1:T(8,128)} %multiply_add_fusion) | data formatting | bytes 16777216 | tf_op jit(solution)/shard_map/add | solution.py:11
  189.6 25.5 %scatter_custom_fusion.3 = f32[513,512]{1,0:T(8,128)S(1)} fusion(s32[4096]{0:T(1024)S(1)} %bitcast.67, f32[4096,512]{1,0:T(8,128)} %copy.43, f32[]{:T(128)} %constant.18.clone.1), kind=kCustom, calls=%fused_computation.49 | custom fusion | flops 2097152 | bytes 1051136 | tf_op jit(solution)/shard_map/scatter-add | solution.py:123
  216.1 7.2 %all_gather.15 = bf16[512,512]{1,0:T(8,128)(2,1)S(1)} all-gather(bf16[512,128]{1,0:T(8,128)(2,1)S(1)} %copy-done.10), channel_id=1, replica_groups=mesh['lat'=8,'lon'=4] {'lon'}, dimensions={1}, use_global_device_ids=true | all-gather | bytes 655360 | tf_op jit(solution)/shard_map/all_gather | solution.py:125
  223.3 30.2 %all-reduce.5.cloned.1.call-done = bf16[512,512]{1,0:T(8,128)(2,1)} async-done(((bf16[512,512]{1,0:T(8,128)(2,1)}), bf16[512,512]{1,0:T(8,128)(2,1)}) %all-reduce.5.cloned.1.call-update) | async-done | bytes 524304 | tf_op jit(solution)/shard_map/psum | solution.py:124
  258.1 31.5 %all-reduce.7.cloned.1.call-done = bf16[512,512]{1,0:T(8,128)(2,1)} async-done(((bf16[512,512]{1,0:T(8,128)(2,1)}), bf16[512,512]{1,0:T(8,128)(2,1)}) %all-reduce.7.cloned.1.call-update) | async-done | bytes 524304 | tf_op jit(solution)/shard_map/psum | solution.py:32
  296.2 5.5 %all-to-all-start.3 = ((bf16[8,64,512]{2,1,0:T(8,128)(2,1)}), bf16[8,64,512]{2,1,0:T(8,128)(2,1)S(1)}, u32[]{:S(2)}, u32[]{:S(2)}) async-start(bf16[8,64,512]{2,1,0:T(8,128)(2,1)} %bitcast.17), calls=%async_computation.3 | async-start | bytes 1048576 | tf_op jit(solution)/shard_map/all_to_all | solution.py:130
  301.8 10.7 %all_gather.19 = bf16[512,512]{1,0:T(8,128)(2,1)} all-gather(bf16[512,128]{1,0:T(8,128)(2,1)S(1)} %copy-done.11), channel_id=1, replica_groups=mesh['lat'=8,'lon'=4] {'lon'}, dimensions={1}, use_global_device_ids=true | all-gather | bytes 655360 | tf_op jit(solution)/shard_map/all_gather | solution.py:135
  317.0 5.1 %gather_fusion.2 = bf16[1024,512]{1,0:T(8,128)(2,1)} fusion(bf16[512,512]{1,0:T(8,128)(2,1)S(1)} %fusion.13, s32[1024]{0:T(1024)S(1)} %fusion.57), kind=kCustom, calls=%fused_computation.3 | custom fusion | bytes 2101248 | tf_op jit(solution)/shard_map/gather | solution.py:133
  322.2 4.0 gather_fusion.1
  329.3 4.3 %fusion.73 = (f32[1024]{0:T(1024)S(1)}, f32[1024,512]{0,1:T(8,128)S(1)}) fusion(bf16[512,512]{1,0:T(8,128)(2,1)S(1)} %copy-done.7, f32[1024,512]{1,0:T(8,128)} %fusion.29, f32[1024,512]{1,0:T(8,128)} %fusion.27, bf16[1024,512]{1,0:T(8,128)(2,1)} %gather_fusion.2, f32[512]{0:T(512)S(1)} %bitcast.75, bf16[1536,512]{1,0:T(8,128)(2,1)} %all-gather.2.cloned.1.call-done), kind=kOutput, calls=%fused_computation.113 | convolution fusion | flops 1078459392 | bytes 8394752 | tf_op jit(solution)/shard_map/dot_general | solution.py:145
  337.9 33.4 %all-reduce.9.cloned.1.call-done = bf16[512,512]{1,0:T(8,128)(2,1)} async-done(((bf16[512,512]{1,0:T(8,128)(2,1)}), bf16[512,512]{1,0:T(8,128)(2,1)}) %all-reduce.9.cloned.1.call-update) | async-done | bytes 524304 | tf_op jit(solution)/shard_map/psum | solution.py:154
  376.0 31.5 %all-reduce.11.cloned.1.call-done = bf16[512,512]{1,0:T(8,128)(2,1)} async-done(((bf16[512,512]{1,0:T(8,128)(2,1)}), bf16[512,512]{1,0:T(8,128)(2,1)}) %all-reduce.11.cloned.1.call-update) | async-done | bytes 524304 | tf_op jit(solution)/shard_map/psum | solution.py:32
  (121 shorter events, 44.3 us)
Async XLA Ops:
  7.2 21.9 %copy-start = (bf16[512,512]{1,0:T(8,128)(2,1)S(1)}, bf16[512,512]{1,0:T(8,128)(2,1)}, u32[]{:S(2)}) copy-start(bf16[512,512]{1,0:T(8,128)(2,1)} %param.27) | copy-start | bytes 1572868
  21.0 29.3 %all-to-all-start = ((s32[8,1,512]{2,1,0:T(1,128)}), s32[8,1,512]{2,1,0:T(1,128)S(1)}, u32[]{:S(2)}, u32[]{:S(2)}) async-start(s32[8,1,512]{2,1,0:T(1,128)} %bitcast.5), calls=%async_computation | async-start | bytes 32768 | tf_op jit(solution)/shard_map/all_to_all | solution.py:112
  50.3 98.9 %all-to-all-start.1 = ((bf16[8,512,512]{2,1,0:T(8,128)(2,1)}), bf16[8,512,512]{2,1,0:T(8,128)(2,1)}, u32[]{:S(2)}, u32[]{:S(2)}) async-start(bf16[8,512,512]{2,1,0:T(8,128)(2,1)} %bitcast.57), calls=%async_computation.1 | async-start | bytes 8388608 | tf_op jit(solution)/shard_map/all_to_all | solution.py:98
  56.5 21.9 %copy-start.13 = (f32[2,512]{1,0:T(2,128)S(1)}, f32[2,512]{1,0:T(2,128)}, u32[]{:S(2)}) copy-start(f32[2,512]{1,0:T(2,128)} %param.40) | copy-start | bytes 12292
  56.5 21.9 %copy-start.14 = (f32[2,512]{1,0:T(2,128)S(1)}, f32[2,512]{1,0:T(2,128)}, u32[]{:S(2)}) copy-start(f32[2,512]{1,0:T(2,128)} %param.44) | copy-start | bytes 12292
  149.2 11.6 %all-to-all-start.2 = ((bf16[8,512,4]{1,2,0:T(4,128)(2,1)}), bf16[8,512,4]{1,2,0:T(4,128)(2,1)S(1)}, u32[]{:S(2)}, u32[]{:S(2)}) async-start(bf16[8,512,4]{1,2,0:T(4,128)(2,1)} %copy.42), calls=%async_computation.2 | async-start | bytes 65536 | tf_op jit(solution)/shard_map/all_to_all | solution.py:105
  152.8 100.7 %all-reduce.5.cloned.1.call-start = ((), (), s32[]{:S(2)}) async-start(), calls=%async_computation.4 | async-start | bytes 1048576 | tf_op jit(solution)/shard_map/psum | solution.py:124
  189.6 26.5 %copy-start.10 = (bf16[512,128]{1,0:T(8,128)(2,1)S(1)}, bf16[512,128]{1,0:T(8,128)(2,1)}, u32[]{:S(2)}) copy-start(bf16[512,128]{1,0:T(8,128)(2,1)} %param.32) | copy-start | bytes 393220
  189.6 63.9 %copy-start.23 = (bf16[1024,128]{1,0:T(8,128)(2,1)S(1)}, bf16[1024,128]{1,0:T(8,128)(2,1)}, u32[]{:S(2)}) copy-start(bf16[1024,128]{1,0:T(8,128)(2,1)} %param.42) | copy-start | bytes 786436
  189.6 63.9 %copy-start.25 = (bf16[128,512]{1,0:T(8,128)(2,1)S(1)}, bf16[128,512]{1,0:T(8,128)(2,1)}, u32[]{:S(2)}) copy-start(bf16[128,512]{1,0:T(8,128)(2,1)} %param.43) | copy-start | bytes 393220
  216.0 73.6 %all-reduce.7.cloned.1.call-start = ((), (), s32[]{:S(2)}) async-start(), calls=%async_computation.5 | async-start | bytes 1048576 | tf_op jit(solution)/shard_map/psum | solution.py:32
  223.3 33.4 %copy-start.15 = (s32[8,64]{1,0:T(8,128)S(1)}, s32[8,64]{1,0:T(8,128)}, u32[]{:S(2)}) copy-start(s32[8,64]{1,0:T(8,128)} %param.34) | copy-start | bytes 6148
  223.3 33.5 %copy-start.3 = (bf16[1024,512]{1,0:T(8,128)(2,1)S(1)}, bf16[1024,512]{1,0:T(8,128)(2,1)}, u32[]{:S(2)}) copy-start(bf16[1024,512]{1,0:T(8,128)(2,1)} %param.33) | copy-start | bytes 3145732
  255.9 36.2 %copy-start.22 = (f32[512]{0:T(512)S(1)}, f32[512]{0:T(512)}, u32[]{:S(2)}) copy-start(f32[512]{0:T(512)} %param.45) | copy-start | bytes 6148
  255.9 58.0 %all-gather.2.cloned.1.call-start = ((), (), s32[]{:S(2)}) async-start(), calls=%async_computation.6 | async-start | bytes 1966080 | tf_op jit(solution)/shard_map/all_gather | solution.py:134
  293.5 19.0 %copy-start.18 = (s32[1024]{0:T(1024)S(1)}, s32[1024]{0:T(1024)}, u32[]{:S(2)}) copy-start(s32[1024]{0:T(1024)} %param.36) | copy-start | bytes 12292
  293.5 19.0 %copy-start.17 = (f32[2,512]{1,0:T(2,128)S(1)}, f32[2,512]{1,0:T(2,128)}, u32[]{:S(2)}) copy-start(f32[2,512]{1,0:T(2,128)} %param.48) | copy-start | bytes 12292
  296.2 25.9 %all-to-all-start.3 = ((bf16[8,64,512]{2,1,0:T(8,128)(2,1)}), bf16[8,64,512]{2,1,0:T(8,128)(2,1)S(1)}, u32[]{:S(2)}, u32[]{:S(2)}) async-start(bf16[8,64,512]{2,1,0:T(8,128)(2,1)} %bitcast.17), calls=%async_computation.3 | async-start | bytes 1048576 | tf_op jit(solution)/shard_map/all_to_all | solution.py:130
  301.7 69.7 %all-reduce.9.cloned.1.call-start = ((), (), s32[]{:S(2)}) async-start(), calls=%async_computation.7 | async-start | bytes 1048576 | tf_op jit(solution)/shard_map/psum | solution.py:154
  336.3 35.1 %copy-start.24 = (bf16[1024,128]{1,0:T(8,128)(2,1)S(1)}, bf16[1024,128]{1,0:T(8,128)(2,1)}, u32[]{:S(2)}) copy-start(bf16[1024,128]{1,0:T(8,128)(2,1)} %param.50) | copy-start | bytes 786436
  336.3 35.1 %copy-start.26 = (bf16[128,512]{1,0:T(8,128)(2,1)S(1)}, bf16[128,512]{1,0:T(8,128)(2,1)}, u32[]{:S(2)}) copy-start(bf16[128,512]{1,0:T(8,128)(2,1)} %param.51) | copy-start | bytes 393220
  337.8 69.7 %all-reduce.11.cloned.1.call-start = ((), (), s32[]{:S(2)}) async-start(), calls=%async_computation.8 | async-start | bytes 1048576 | tf_op jit(solution)/shard_map/psum | solution.py:32
  337.9 36.8 %copy-start.6 = (bf16[1024,512]{0,1:T(8,128)(2,1)S(1)}, bf16[1024,512]{0,1:T(8,128)(2,1)}, u32[]{:S(2)}) copy-start(bf16[1024,512]{0,1:T(8,128)(2,1)} %copy-done.5) | copy-start | bytes 3145732
  373.9 37.0 %copy-start.1 = (bf16[512,512]{1,0:T(8,128)(2,1)S(1)}, bf16[512,512]{1,0:T(8,128)(2,1)}, u32[]{:S(2)}) copy-start(bf16[512,512]{1,0:T(8,128)(2,1)} %param.27) | copy-start | bytes 1572868
  (13 other events, 66.2 us)
Sparse Core Ops, SparseCore 0:
  216.1 37.3 all-reduce.4
  256.1 33.4 all-reduce.6
  291.2 22.7 all-gather.1
  338.0 33.3 all-reduce.8
  374.0 33.5 all-reduce.10
where the time goes:
time: 419 us; the launch traced here: 417 us
  waiting for transfers between devices  199 us (47%)
  local copies, waits for them, and re-layouts  66.1 us (16%)
  other arithmetic  48.8 us (12%)
  matrix products  33.5 us (8%)
  blocking collectives  32.4 us (8%)
  starting transfers between devices  23.2 us (6%)
  between operations  14.2 us (3%)
    all_to_all x1, waiting for transfers between devices, local(): lax.all_to_all(row_buffer.reshape(lat_count, capacity, feature_width), 'l...  70.7 us
    psum x2, waiting for transfers between devices, node_network(): lax.psum(jnp.dot(hidden, weight_out, preferred_element_type=jnp.float32)....  63 us
    psum x1, waiting for transfers between devices, local(): lax.psum(jnp.dot(edge_onehot, edge_update, preferred_element_type=jnp.flo...  33.4 us
    psum x1, waiting for transfers between devices, local(): gathered = lax.psum(partial_sum.astype(jnp.bfloat16), 'lon')  30.2 us
    scatter-add x1, other arithmetic, local(): jax.ops.segment_sum(arrived, segment_ids, num_segments=mesh_rows + 1)  25.5 us
    scatter x1, local copies, waits for them, and re-layouts, local(): row_buffer = jnp.zeros((slot_total, feature_width), jnp.bfloat16).at[slot...  21.3 us
    all_gather x1, blocking collectives, local(): piece_out = lax.all_gather(proc_edge_out, 'lon', axis=1, tiled=True)  10.7 us
    add x1, local copies, waits for them, and re-layouts, layer_norm(): return centred * lax.rsqrt(spread + 1e-05) * norm_gain + offsets  8.98 us
  transfers between devices with their start and end apart: 9, of which 6 were waited for; matrix products, arithmetic and copies ran while one was open for 13% of the time, Pallas kernels for 0%

commit v1 on v0

--- a/solution.py
+++ b/solution.py
@@ -23,14 +23,18 @@
 
 
 def node_network(base, aggregate, weight_in, weight_out, biases, norm_gain):
+
+    def screen_note(here_x):
+        return jnp.sum(lax.all_gather(here_x, "lon"), 0)
+
     inputs = jnp.concatenate([base, aggregate], 1)
     columns = weight_in.shape[1]
     hidden_bias = lax.dynamic_slice_in_dim(biases[0], lax.axis_index("lon") * columns, columns)
     hidden = jax.nn.silu(
         jnp.dot(inputs, weight_in, preferred_element_type=jnp.float32) + hidden_bias
     ).astype(jnp.bfloat16)
-    raw_out = lax.psum(
-        jnp.dot(hidden, weight_out, preferred_element_type=jnp.float32).astype(jnp.bfloat16), "lon"
+    raw_out = screen_note(
+        jnp.dot(hidden, weight_out, preferred_element_type=jnp.float32).astype(jnp.bfloat16)
     ).astype(jnp.float32)
     return (base.astype(jnp.float32) + layer_norm(raw_out, norm_gain, biases[1])).astype(
         jnp.bfloat16

time: 419 us -> 397 us (0.947)
  waiting for transfers between devices: 199 us -> 178 us
    psum x2 -> x0, waiting for transfers between devices: 63 us -> none  [node_network(): lax.psum(jnp.dot(hidden, weight_out, preferred_element_type=jnp.float32)....]
    all_gather x0 -> x2, waiting for transfers between devices: none -> 41.3 us  [screen_note(): return jnp.sum(lax.all_gather(here_x, 'lon'), 0)]
    reduce_sum x0 -> x2, other arithmetic: none -> 4.41 us  [screen_note(): return jnp.sum(lax.all_gather(here_x, 'lon'), 0)]
  transfers between devices with their start and end apart: 9 -> 9, of which waited for: 6 -> 6; matrix products, arithmetic and copies ran while one was open for 13% -> 14% of each run, Pallas kernels for 0% -> 0%
where the time goes in v1:
time: 397 us; the launch traced here: 396 us
  waiting for transfers between devices  178 us (45%)
  local copies, waits for them, and re-layouts  66.1 us (17%)
  other arithmetic  48 us (12%)
  matrix products  33.5 us (8%)
  blocking collectives  32.6 us (8%)
  starting transfers between devices  23.2 us (6%)
  between operations  14.2 us (4%)
    all_to_all x1, waiting for transfers between devices, local(): lax.all_to_all(row_buffer.reshape(lat_count, capacity, feature_width), 'l...  70.7 us
    all_gather x2, waiting for transfers between devices, screen_note(): return jnp.sum(lax.all_gather(here_x, 'lon'), 0)  41.3 us
    psum x1, waiting for transfers between devices, local(): lax.psum(jnp.dot(edge_onehot, edge_update, preferred_element_type=jnp.flo...  33.5 us
    psum x1, waiting for transfers between devices, local(): gathered = lax.psum(partial_sum.astype(jnp.bfloat16), 'lon')  30.2 us
    scatter-add x1, other arithmetic, local(): jax.ops.segment_sum(arrived, segment_ids, num_segments=mesh_rows + 1)  25.5 us
    scatter x1, local copies, waits for them, and re-layouts, local(): row_buffer = jnp.zeros((slot_total, feature_width), jnp.bfloat16).at[slot...  21.3 us
    all_gather x1, blocking collectives, local(): piece_out = lax.all_gather(proc_edge_out, 'lon', axis=1, tiled=True)  10.9 us
    add x1, local copies, waits for them, and re-layouts, layer_norm(): return centred * lax.rsqrt(spread + 1e-05) * norm_gain + offsets  8.98 us
  transfers between devices with their start and end apart: 9, of which 6 were waited for; matrix products, arithmetic and copies ran while one was open for 14% of the time, Pallas kernels for 0%

profile of v1, /device:TPU:0, one launch (start us, length us, event | category | flops | bytes accessed | tf_op | source)
XLA Modules:
  0.0 395.8 jit_solution(5510590718619167925)
XLA Ops:
  12.2 8.8 %scatter_custom_fusion = s32[4096]{0:T(1024)} fusion(s32[2048]{0:T(1024)S(1)} %bitcast.75, s32[2048]{0:T(1024)} %param.31, s32[]{:T(128)} %constant.21.clone.1), kind=kCustom, calls=%fused_computation.87 | custom fusion | bytes 16896 | tf_op jit(solution)/shard_map/scatter | solution.py:90
  21.0 7.3 %all-to-all-start = ((s32[8,1,512]{2,1,0:T(1,128)}), s32[8,1,512]{2,1,0:T(1,128)S(1)}, u32[]{:S(2)}, u32[]{:S(2)}) async-start(s32[8,1,512]{2,1,0:T(1,128)} %bitcast.5), calls=%async_computation | async-start | bytes 32768 | tf_op jit(solution)/shard_map/all_to_all | solution.py:116
  29.0 21.3 %scatter_custom_fusion.1 = bf16[4096,512]{1,0:T(8,128)(2,1)} fusion(s32[2048]{0:T(1024)S(1)} %bitcast.76, bf16[512,512]{1,0:T(8,128)(2,1)S(1)} %copy-done, s32[2048]{0:T(1024)S(1)} %fusion.53, bf16[]{:T(256)} %constant.25.clone.1), kind=kCustom, calls=%fused_computation.11 | custom fusion | bytes 4194306 | tf_op jit(solution)/shard_map/scatter | solution.py:96
  50.3 6.1 %all-to-all-start.1 = ((bf16[8,512,512]{2,1,0:T(8,128)(2,1)}), bf16[8,512,512]{2,1,0:T(8,128)(2,1)}, u32[]{:S(2)}, u32[]{:S(2)}) async-start(bf16[8,512,512]{2,1,0:T(8,128)(2,1)} %bitcast.59), calls=%async_computation.1 | async-start | bytes 8388608 | tf_op jit(solution)/shard_map/all_to_all | solution.py:102
  56.8 6.1 %scatter_custom_fusion.2 = bf16[4096,4]{1,0:T(8,128)(2,1)S(1)} fusion(s32[2048]{0:T(1024)S(1)} %bitcast.77, bf16[2048,4]{1,0:T(8,128)(2,1)S(1)} %copy.41, bf16[]{:T(256)} %constant.25.clone.1), kind=kCustom, calls=%fused_computation.56 | custom fusion | bytes 32770 | tf_op jit(solution)/shard_map/scatter | solution.py:99
  63.9 7.2 %all_gather.28 = bf16[512,512]{1,0:T(8,128)(2,1)S(1)} all-gather(bf16[512,128]{1,0:T(8,128)(2,1)S(1)} %copy-done.8), channel_id=1, replica_groups=mesh['lat'=8,'lon'=4] {'lon'}, dimensions={1}, use_global_device_ids=true | all-gather | bytes 655360 | tf_op jit(solution)/shard_map/all_gather | solution.py:15
  71.1 7.3 %all_gather.29 = bf16[512,512]{1,0:T(8,128)(2,1)S(1)} all-gather(bf16[512,128]{1,0:T(8,128)(2,1)S(1)} %copy-done.9), channel_id=1, replica_groups=mesh['lat'=8,'lon'=4] {'lon'}, dimensions={1}, use_global_device_ids=true | all-gather | bytes 655360 | tf_op jit(solution)/shard_map/all_gather | solution.py:16
  78.4 70.7 %all-to-all-done.1 = bf16[8,512,512]{2,1,0:T(8,128)(2,1)} async-done(((bf16[8,512,512]{2,1,0:T(8,128)(2,1)}), bf16[8,512,512]{2,1,0:T(8,128)(2,1)}, u32[]{:S(2)}, u32[]{:S(2)}) %all-to-all-start.1) | async-done | bytes 4194336 | tf_op jit(solution)/shard_map/all_to_all | solution.py:102
  153.0 7.7 %fusion.76 = f32[4096,512]{1,0:T(8,128)} fusion(bf16[4096,512]{1,0:T(8,128)(2,1)} %bitcast.9, bf16[512,512]{1,0:T(8,128)(2,1)S(1)} %all_gather.28), kind=kOutput, calls=%fused_computation.114 | convolution fusion | flops 2147483648 | bytes 13107200 | tf_op jit(solution)/shard_map/dot_general | solution.py:17
  160.8 8.9 %fusion.72 = (f32[4096]{0:T(1024)S(1)}, f32[4096,512]{0,1:T(8,128)}) fusion(bf16[512,512]{1,0:T(8,128)(2,1)S(1)} %all_gather.29, f32[4096,512]{1,0:T(8,128)} %fusion.76, bf16[4096,4]{0,1:T(4,128)(2,1)S(1)} %bitcast.68, bf16[4,512]{1,0:T(4,128)(2,1)S(1)} %copy-done.27, f32[512]{0:T(512)S(1)} %bitcast.78), kind=kOutput, calls=%fused_computation.112 | convolution fusion | flops 2181033984 | bytes 17356800 | tf_op jit(solution)/shard_map/dot_general | solution.py:20
  169.7 4.5 %multiply_reduce_fusion = f32[4096]{0:T(1024)S(1)} fusion(f32[4096,512]{0,1:T(8,128)} %get-tuple-element.21, f32[4096]{0:T(1024)S(1)} %broadcast_multiply_fusion), kind=kLoop, calls=%fused_computation.9 | loop fusion | flops 6287360 | bytes 8421376 | tf_op jit(solution)/shard_map/reduce_sum | solution.py:10
  175.5 5.1 %multiply_add_fusion = f32[4096,512]{0,1:T(8,128)} fusion(f32[4096,512]{0,1:T(8,128)S(1)} %copy-done.2, f32[512]{0:T(512)S(1)} %bitcast.74, f32[512]{0:T(512)S(1)} %copy-done.21, f32[4096]{0:T(1024)S(1)} %add_rsqrt_fusion, f32[4096]{0:T(1024)S(1)} %broadcast_multiply_fusion), kind=kLoop, calls=%fused_computation.8 | loop fusion | flops 8388608 | bytes 16814080 | tf_op jit(solution)/shard_map/add | solution.py:11
  180.6 9.0 %copy.43 = f32[4096,512]{1,0:T(8,128)} copy(f32[4096,512]{0,1:T(8,128)} %multiply_add_fusion) | data formatting | bytes 16777216 | tf_op jit(solution)/shard_map/add | solution.py:11
  189.6 25.5 %scatter_custom_fusion.3 = f32[513,512]{1,0:T(8,128)S(1)} fusion(s32[4096]{0:T(1024)S(1)} %bitcast.71, f32[4096,512]{1,0:T(8,128)} %copy.43, f32[]{:T(128)} %constant.20.clone.1), kind=kCustom, calls=%fused_computation.49 | custom fusion | flops 2097152 | bytes 1051136 | tf_op jit(solution)/shard_map/scatter-add | solution.py:127
  216.1 7.2 %all_gather.27 = bf16[512,512]{1,0:T(8,128)(2,1)S(1)} all-gather(bf16[512,128]{1,0:T(8,128)(2,1)S(1)} %copy-done.10), channel_id=1, replica_groups=mesh['lat'=8,'lon'=4] {'lon'}, dimensions={1}, use_global_device_ids=true | all-gather | bytes 655360 | tf_op jit(solution)/shard_map/all_gather | solution.py:129
  223.3 30.2 %all-reduce.3.cloned.1.call-done = bf16[512,512]{1,0:T(8,128)(2,1)} async-done(((bf16[512,512]{1,0:T(8,128)(2,1)}), bf16[512,512]{1,0:T(8,128)(2,1)}) %all-reduce.3.cloned.1.call-update) | async-done | bytes 524304 | tf_op jit(solution)/shard_map/psum | solution.py:128
  258.1 20.6 %all-gather.8.cloned.1.call-done = bf16[2048,512]{1,0:T(8,128)(2,1)} async-done(((bf16[512,512]{1,0:T(8,128)(2,1)}), bf16[2048,512]{1,0:T(8,128)(2,1)}) %all-gather.8.cloned.1.call-update) | async-done | bytes 2097168 | tf_op jit(solution)/shard_map/all_gather | solution.py:28
  284.4 5.5 %all-to-all-start.3 = ((bf16[8,64,512]{2,1,0:T(8,128)(2,1)}), bf16[8,64,512]{2,1,0:T(8,128)(2,1)S(1)}, u32[]{:S(2)}, u32[]{:S(2)}) async-start(bf16[8,64,512]{2,1,0:T(8,128)(2,1)} %bitcast.18), calls=%async_computation.3 | async-start | bytes 1048576 | tf_op jit(solution)/shard_map/all_to_all | solution.py:134
  290.0 10.9 %all_gather.33 = bf16[512,512]{1,0:T(8,128)(2,1)} all-gather(bf16[512,128]{1,0:T(8,128)(2,1)S(1)} %copy-done.11), channel_id=1, replica_groups=mesh['lat'=8,'lon'=4] {'lon'}, dimensions={1}, use_global_device_ids=true | all-gather | bytes 655360 | tf_op jit(solution)/shard_map/all_gather | solution.py:139
  306.1 5.1 %gather_fusion.2 = bf16[1024,512]{1,0:T(8,128)(2,1)} fusion(bf16[512,512]{1,0:T(8,128)(2,1)S(1)} %fusion.13, s32[1024]{0:T(1024)S(1)} %fusion.57), kind=kCustom, calls=%fused_computation.3 | custom fusion | bytes 2101248 | tf_op jit(solution)/shard_map/gather | solution.py:137
  311.2 4.0 %gather_fusion.1 = bf16[1024,512]{1,0:T(8,128)(2,1)S(1)} fusion(bf16[1024,512]{1,0:T(8,128)(2,1)S(1)} %pad_maximum_fusion, s32[1024]{0:T(1024)S(1)} %fusion.56), kind=kCustom, calls=%fused_computation.2 | custom fusion | bytes 2101248 | tf_op jit(solution)/shard_map/gather | solution.py:136
  318.3 4.3 %fusion.73 = (f32[1024]{0:T(1024)S(1)}, f32[1024,512]{0,1:T(8,128)S(1)}) fusion(bf16[512,512]{1,0:T(8,128)(2,1)S(1)} %copy-done.7, f32[1024,512]{1,0:T(8,128)} %fusion.29, f32[1024,512]{1,0:T(8,128)} %fusion.27, bf16[1024,512]{1,0:T(8,128)(2,1)} %gather_fusion.2, f32[512]{0:T(512)S(1)} %bitcast.79, bf16[1536,512]{1,0:T(8,128)(2,1)} %all-gather.6.cloned.1.call-done), kind=kOutput, calls=%fused_computation.113 | convolution fusion | flops 1078459392 | bytes 8394752 | tf_op jit(solution)/shard_map/dot_general | solution.py:149
  327.0 33.5 %all-reduce.5.cloned.1.call-done = bf16[512,512]{1,0:T(8,128)(2,1)} async-done(((bf16[512,512]{1,0:T(8,128)(2,1)}), bf16[512,512]{1,0:T(8,128)(2,1)}) %all-reduce.5.cloned.1.call-update) | async-done | bytes 524304 | tf_op jit(solution)/shard_map/psum | solution.py:158
  365.1 20.7 %all-gather.10.cloned.1.call-done = bf16[2048,512]{1,0:T(8,128)(2,1)} async-done(((bf16[512,512]{1,0:T(8,128)(2,1)}), bf16[2048,512]{1,0:T(8,128)(2,1)}) %all-gather.10.cloned.1.call-update) | async-done | bytes 2097168 | tf_op jit(solution)/shard_map/all_gather | solution.py:28
  (123 shorter events, 44.1 us)
Async XLA Ops:
  7.2 21.9 %copy-start = (bf16[512,512]{1,0:T(8,128)(2,1)S(1)}, bf16[512,512]{1,0:T(8,128)(2,1)}, u32[]{:S(2)}) copy-start(bf16[512,512]{1,0:T(8,128)(2,1)} %param.27) | copy-start | bytes 1572868
  21.0 29.3 %all-to-all-start = ((s32[8,1,512]{2,1,0:T(1,128)}), s32[8,1,512]{2,1,0:T(1,128)S(1)}, u32[]{:S(2)}, u32[]{:S(2)}) async-start(s32[8,1,512]{2,1,0:T(1,128)} %bitcast.5), calls=%async_computation | async-start | bytes 32768 | tf_op jit(solution)/shard_map/all_to_all | solution.py:116
  50.3 98.9 %all-to-all-start.1 = ((bf16[8,512,512]{2,1,0:T(8,128)(2,1)}), bf16[8,512,512]{2,1,0:T(8,128)(2,1)}, u32[]{:S(2)}, u32[]{:S(2)}) async-start(bf16[8,512,512]{2,1,0:T(8,128)(2,1)} %bitcast.59), calls=%async_computation.1 | async-start | bytes 8388608 | tf_op jit(solution)/shard_map/all_to_all | solution.py:102
  56.4 14.7 %copy-start.9 = (bf16[512,128]{1,0:T(8,128)(2,1)S(1)}, bf16[512,128]{1,0:T(8,128)(2,1)}, u32[]{:S(2)}) copy-start(bf16[512,128]{1,0:T(8,128)(2,1)} %param.39) | copy-start | bytes 393220
  56.5 21.9 %copy-start.13 = (f32[2,512]{1,0:T(2,128)S(1)}, f32[2,512]{1,0:T(2,128)}, u32[]{:S(2)}) copy-start(f32[2,512]{1,0:T(2,128)} %param.40) | copy-start | bytes 12292
  56.5 21.9 %copy-start.14 = (f32[2,512]{1,0:T(2,128)S(1)}, f32[2,512]{1,0:T(2,128)}, u32[]{:S(2)}) copy-start(f32[2,512]{1,0:T(2,128)} %param.44) | copy-start | bytes 12292
  149.2 11.6 %all-to-all-start.2 = ((bf16[8,512,4]{1,2,0:T(4,128)(2,1)}), bf16[8,512,4]{1,2,0:T(4,128)(2,1)S(1)}, u32[]{:S(2)}, u32[]{:S(2)}) async-start(bf16[8,512,4]{1,2,0:T(4,128)(2,1)} %copy.42), calls=%async_computation.2 | async-start | bytes 65536 | tf_op jit(solution)/shard_map/all_to_all | solution.py:109
  152.8 100.7 %all-reduce.3.cloned.1.call-start = ((), (), s32[]{:S(2)}) async-start(), calls=%async_computation.4 | async-start | bytes 1048576 | tf_op jit(solution)/shard_map/psum | solution.py:128
  189.6 26.5 %copy-start.10 = (bf16[512,128]{1,0:T(8,128)(2,1)S(1)}, bf16[512,128]{1,0:T(8,128)(2,1)}, u32[]{:S(2)}) copy-start(bf16[512,128]{1,0:T(8,128)(2,1)} %param.32) | copy-start | bytes 393220
  189.6 63.9 %copy-start.23 = (bf16[1024,128]{1,0:T(8,128)(2,1)S(1)}, bf16[1024,128]{1,0:T(8,128)(2,1)}, u32[]{:S(2)}) copy-start(bf16[1024,128]{1,0:T(8,128)(2,1)} %param.42) | copy-start | bytes 786436
  189.6 63.9 %copy-start.25 = (bf16[128,512]{1,0:T(8,128)(2,1)S(1)}, bf16[128,512]{1,0:T(8,128)(2,1)}, u32[]{:S(2)}) copy-start(bf16[128,512]{1,0:T(8,128)(2,1)} %param.43) | copy-start | bytes 393220
  216.0 62.7 %all-gather.8.cloned.1.call-start = ((), (), s32[]{:S(2)}) async-start(), calls=%async_computation.7 | async-start | bytes 2621440 | tf_op jit(solution)/shard_map/all_gather | solution.py:28
  223.3 33.4 %copy-start.15 = (s32[8,64]{1,0:T(8,128)S(1)}, s32[8,64]{1,0:T(8,128)}, u32[]{:S(2)}) copy-start(s32[8,64]{1,0:T(8,128)} %param.34) | copy-start | bytes 6148
  223.3 33.5 %copy-start.3 = (bf16[1024,512]{1,0:T(8,128)(2,1)S(1)}, bf16[1024,512]{1,0:T(8,128)(2,1)}, u32[]{:S(2)}) copy-start(bf16[1024,512]{1,0:T(8,128)(2,1)} %param.33) | copy-start | bytes 3145732
  255.9 47.0 %all-gather.6.cloned.1.call-start = ((), (), s32[]{:S(2)}) async-start(), calls=%async_computation.5 | async-start | bytes 1966080 | tf_op jit(solution)/shard_map/all_gather | solution.py:138
  258.1 23.3 %copy-start.22 = (f32[512]{0:T(512)S(1)}, f32[512]{0:T(512)}, u32[]{:S(2)}) copy-start(f32[512]{0:T(512)} %param.45) | copy-start | bytes 6148
  281.8 19.1 %copy-start.18 = (s32[1024]{0:T(1024)S(1)}, s32[1024]{0:T(1024)}, u32[]{:S(2)}) copy-start(s32[1024]{0:T(1024)} %param.36) | copy-start | bytes 12292
  281.8 19.1 %copy-start.17 = (f32[2,512]{1,0:T(2,128)S(1)}, f32[2,512]{1,0:T(2,128)}, u32[]{:S(2)}) copy-start(f32[2,512]{1,0:T(2,128)} %param.48) | copy-start | bytes 12292
  284.4 26.7 %all-to-all-start.3 = ((bf16[8,64,512]{2,1,0:T(8,128)(2,1)}), bf16[8,64,512]{2,1,0:T(8,128)(2,1)S(1)}, u32[]{:S(2)}, u32[]{:S(2)}) async-start(bf16[8,64,512]{2,1,0:T(8,128)(2,1)} %bitcast.18), calls=%async_computation.3 | async-start | bytes 1048576 | tf_op jit(solution)/shard_map/all_to_all | solution.py:134
  290.0 70.5 %all-reduce.5.cloned.1.call-start = ((), (), s32[]{:S(2)}) async-start(), calls=%async_computation.6 | async-start | bytes 1048576 | tf_op jit(solution)/shard_map/psum | solution.py:158
  325.3 35.2 %copy-start.24 = (bf16[1024,128]{1,0:T(8,128)(2,1)S(1)}, bf16[1024,128]{1,0:T(8,128)(2,1)}, u32[]{:S(2)}) copy-start(bf16[1024,128]{1,0:T(8,128)(2,1)} %param.50) | copy-start | bytes 786436
  325.3 35.2 %copy-start.26 = (bf16[128,512]{1,0:T(8,128)(2,1)S(1)}, bf16[128,512]{1,0:T(8,128)(2,1)}, u32[]{:S(2)}) copy-start(bf16[128,512]{1,0:T(8,128)(2,1)} %param.51) | copy-start | bytes 393220
  326.9 58.9 %all-gather.10.cloned.1.call-start = ((), (), s32[]{:S(2)}) async-start(), calls=%async_computation.8 | async-start | bytes 2621440 | tf_op jit(solution)/shard_map/all_gather | solution.py:28
  327.0 36.8 %copy-start.6 = (bf16[1024,512]{0,1:T(8,128)(2,1)S(1)}, bf16[1024,512]{0,1:T(8,128)(2,1)}, u32[]{:S(2)}) copy-start(bf16[1024,512]{0,1:T(8,128)(2,1)} %copy-done.5) | copy-start | bytes 3145732
  (13 other events, 55.0 us)
Sparse Core Ops, SparseCore 0:
  216.1 37.3 all-reduce.2
  256.1 22.6 all-gather.7
  280.3 22.6 all-gather.5
  327.0 33.4 all-reduce.4
  363.0 22.6 all-gather.9
